TPU v7x, 128 devices: a whole 4x4x4 slice. The times are simulated.
128 devices in a mesh: dom: 4 (over y_hi, core), dim: 32 (over z, y_lo, x).
Axes of the slice: x: 4, y: 4 (y_hi: 2, y_lo: 2; y = y_hi * 2 + y_lo), z: 4, core: 2. Of those that a mesh axis runs over, the one named last changes fastest.
Arguments:
- particles: float32 [512, 262144], P('dom', 'dim'), may hold values from -16 to 16
- scores: float32 [512, 262144], P('dom', 'dim'), may hold values from -0.00036621094 to 0.00036621094
- spread: float32 [], replicated, may hold values from 131072 to 262144
- step_size: float32 [], replicated, may hold values from 4194304 to 8388608
Outputs:
- new_particles: float32 [512, 262144], P('dom', 'dim')
All inputs are finite; a program needn't handle non-finite values.
Results may differ from a plain program's by a relative error of at most 0.000064.
Values sent between devices are 32-bit elements; how exact they have to be, the bound alone decides.
A program may use at most 128 MiB of HBM per device.

v0:
```python
import jax
import jax.numpy as jnp
from jax import lax
from jax.sharding import PartitionSpec as P


def cut_along(array, dim, devices):
    dims = array.shape
    blocks = array.reshape(*dims[:dim], devices, dims[dim] // devices, *dims[dim + 1 :])
    return jnp.moveaxis(blocks, dim, 0)


def sum_at_owner(array, axis, dim):
    blocks = cut_along(array, dim, lax.axis_size(axis))
    arrived = lax.all_to_all(blocks, axis, split_axis=0, concat_axis=0, tiled=True)
    return arrived.sum(axis=0)


def from_everyone(array, axis):
    devices = lax.axis_size(axis)
    return lax.all_to_all(
        jnp.broadcast_to(array[None], (devices, *array.shape)), axis, 0, 0, tiled=True
    )


def over_copies(array, axis):
    everything = from_everyone(array, axis)
    return jnp.sum(everything, axis=0)


def in_order(blocks, dim):
    dims = list(blocks.shape[1:])
    dims[dim] *= blocks.shape[0]
    return jnp.moveaxis(blocks, 0, dim).reshape(dims)


def gathered_copies(array, axis, dim):
    return in_order(from_everyone(array, axis), dim)


def on_device(particles, scores, spread, step_size):
    precise = lax.Precision.HIGHEST
    local_rows = particles.shape[0]
    count_all = local_rows * lax.axis_size("dom")
    gathered = lax.all_gather(particles, "dom", axis=0, tiled=True)
    product = lax.dot_general(
        particles,
        gathered,
        (((1,), (1,)), ((), ())),
        precision=precise,
        preferred_element_type=jnp.float32,
    )
    norms = jnp.sum(gathered * gathered, axis=1)
    gram_share, square_share = (sum_at_owner(product, "dim", 1), sum_at_owner(norms, "dim", 0))
    own_squares = over_copies(jnp.sum(particles * particles, axis=1), "dim")
    kernel_share = jnp.exp(
        -(own_squares[:, None] + square_share[None, :] - 2.0 * gram_share) / spread
    )
    kernel = gathered_copies(kernel_share, "dim", 1)
    attract = jnp.dot(
        kernel,
        lax.all_gather(scores, "dom", axis=0, tiled=True),
        precision=precise,
        preferred_element_type=jnp.float32,
    )
    pulled = jnp.dot(kernel, gathered, precision=precise, preferred_element_type=jnp.float32)
    weight_sum = jnp.sum(kernel, axis=1, keepdims=True)
    update = (attract + 2.0 / spread * (weight_sum * particles - pulled)) / count_all
    return particles + step_size * update


def solution(mesh):
    return jax.shard_map(
        on_device,
        mesh=mesh,
        in_specs=(P("dom", "dim"), P("dom", "dim"), P(), P()),
        out_specs=P("dom", "dim"),
        check_vma=False,
    )
```

profile of v0, /device:TPU:1, one launch (start us, length us, event | category | flops | bytes accessed | tf_op | source)
XLA Modules:
  0.0 261.2 jit_solution(14739660811756581120)
XLA Ops:
  6.5 0.0 all-gather.3.cloned.1.call-start
  6.5 0.7 all-gather.3.cloned.1.call-update
  7.3 0.0 all-gather.5.cloned.1.call-start
  7.3 0.7 all-gather.5.cloned.1.call-update
  8.0 2.5 multiply_reduce_fusion.1
  10.5 0.6 broadcast_in_dim.4
  11.2 9.7 %all-to-all-start = ((f32[32,1,128]{2,1,0:T(1,128)}), f32[32,1,128]{2,1,0:T(1,128)S(1)}, u32[]{:S(2)}, u32[]{:S(2)}) async-start(f32[32,1,128]{2,1,0:T(1,128)} %broadcast_in_dim.4), calls=%async_computation | async-start | bytes 32768 | tf_op jit(solution)/shard_map/all_to_all | solution.py:21
  20.9 101.7 %all-gather.3.cloned.1.call-done = f32[512,8192]{1,0:T(8,128)} async-done(((f32[128,8192]{1,0:T(8,128)}), f32[512,8192]{1,0:T(8,128)}) %all-gather.3.cloned.1.call-update) | async-done | bytes 16777232 | tf_op jit(solution)/shard_map/all_gather | solution.py:45
  122.6 7.0 %multiply_reduce_fusion = f32[512]{0:T(512)S(1)} fusion(f32[512,8192]{1,0:T(8,128)} %all-gather.3.cloned.1.call-done), kind=kLoop, calls=%fused_computation | loop fusion | flops 8388096 | bytes 16779264 | tf_op jit(solution)/shard_map/reduce_sum | solution.py:53
  129.6 0.7 all_to_all.17
  130.2 0.0 all-to-all-done
  130.2 7.0 %all-to-all-start.1 = ((f32[32,1,16]{2,1,0:T(1,128)}), f32[32,1,16]{2,1,0:T(1,128)S(1)}, u32[]{:S(2)}, u32[]{:S(2)}) async-start(f32[32,1,16]{2,1,0:T(1,128)} %bitcast.1), calls=%async_computation.1 | async-start | bytes 32768 | tf_op jit(solution)/shard_map/all_to_all | solution.py:15
  137.2 17.7 %fusion.3 = f32[128,512]{0,1:T(8,128)} fusion(f32[128,8192]{1,0:T(8,128)} %param.4, f32[512,8192]{1,0:T(8,128)} %all-gather.3.cloned.1.call-done), kind=kOutput, calls=%fused_computation.8 | convolution fusion | flops 6442450944 | bytes 21233664 | tf_op jit(solution)/shard_map/dot_general | solution.py:46
  155.0 0.0 all-to-all-done.1
  155.0 7.8 %all-to-all-start.2 = ((f32[32,128,16]{1,2,0:T(8,128)}), f32[32,128,16]{1,2,0:T(8,128)S(1)}, u32[]{:S(2)}, u32[]{:S(2)}) async-start(f32[32,128,16]{1,2,0:T(8,128)} %bitcast.3), calls=%async_computation.2 | async-start | bytes 524288 | tf_op jit(solution)/shard_map/all_to_all | solution.py:15
  163.4 0.1 reduce_sum.57
  163.5 7.5 %all-to-all-done.2 = f32[32,128,16]{1,2,0:T(8,128)S(1)} async-done(((f32[32,128,16]{1,2,0:T(8,128)}), f32[32,128,16]{1,2,0:T(8,128)S(1)}, u32[]{:S(2)}, u32[]{:S(2)}) %all-to-all-start.2) | async-done | bytes 262176 | tf_op jit(solution)/shard_map/all_to_all | solution.py:15
  171.0 0.1 divide_exponential_fusion
  171.1 0.7 broadcast_in_dim.5
  171.8 5.5 %all-to-all-start.3 = ((f32[32,128,16]{1,2,0:T(8,128)}), f32[32,128,16]{1,2,0:T(8,128)S(1)}, u32[]{:S(2)}, u32[]{:S(2)}) async-start(f32[32,128,16]{1,2,0:T(8,128)} %broadcast_in_dim.5), calls=%async_computation.3 | async-start | bytes 524288 | tf_op jit(solution)/shard_map/all_to_all | solution.py:21
  178.0 7.3 %all-to-all-done.3 = f32[32,128,16]{1,2,0:T(8,128)S(1)} async-done(((f32[32,128,16]{1,2,0:T(8,128)}), f32[32,128,16]{1,2,0:T(8,128)S(1)}, u32[]{:S(2)}, u32[]{:S(2)}) %all-to-all-start.3) | async-done | bytes 262176 | tf_op jit(solution)/shard_map/all_to_all | solution.py:21
  185.4 0.1 reduce_sum.59
  185.4 14.4 %fusion = f32[128,8192]{1,0:T(8,128)} fusion(f32[128,512]{0,1:T(8,128)S(1)} %bitcast.14, f32[512,8192]{1,0:T(8,128)} %all-gather.3.cloned.1.call-done, f32[128,8192]{1,0:T(8,128)} %param.4, f32[128]{0:T(128)S(1)} %reduce_sum.59, f32[]{:T(128)S(6)} %div.17), kind=kOutput, calls=%fused_computation.2 | convolution fusion | flops 6445596672 | bytes 25428484 | tf_op jit(solution)/shard_map/dot_general | solution.py:66
  199.8 39.6 %all-gather.5.cloned.1.call-done = f32[512,8192]{1,0:T(8,128)} async-done(((f32[128,8192]{1,0:T(8,128)}), f32[512,8192]{1,0:T(8,128)}) %all-gather.5.cloned.1.call-update) | async-done | bytes 16777232 | tf_op jit(solution)/shard_map/all_gather | solution.py:62
  239.4 15.0 %fusion.2 = f32[128,8192]{1,0:T(8,128)} fusion(f32[128,8192]{1,0:T(8,128)} %param.4, f32[128,8192]{1,0:T(8,128)} %fusion, f32[128,512]{0,1:T(8,128)S(1)} %bitcast.15, f32[512,8192]{1,0:T(8,128)} %all-gather.5.cloned.1.call-done, f32[]{:T(128)S(6)} %mul.46), kind=kOutput, calls=%fused_computation.5 | convolution fusion | flops 6445596672 | bytes 29622276 | tf_op jit(solution)/shard_map/dot_general | solution.py:60
  (2 shorter events, 0.1 us)
Async XLA Ops:
  6.5 116.1 %all-gather.3.cloned.1.call-start = ((), (), s32[]{:S(2)}) async-start(), calls=%async_computation.4 | async-start | bytes 20971520 | tf_op jit(solution)/shard_map/all_gather | solution.py:45
  7.3 232.1 %all-gather.5.cloned.1.call-start = ((), (), s32[]{:S(2)}) async-start(), calls=%async_computation.5 | async-start | bytes 20971520 | tf_op jit(solution)/shard_map/all_gather | solution.py:62
  11.2 119.1 %all-to-all-start = ((f32[32,1,128]{2,1,0:T(1,128)}), f32[32,1,128]{2,1,0:T(1,128)S(1)}, u32[]{:S(2)}, u32[]{:S(2)}) async-start(f32[32,1,128]{2,1,0:T(1,128)} %broadcast_in_dim.4), calls=%async_computation | async-start | bytes 32768 | tf_op jit(solution)/shard_map/all_to_all | solution.py:21
  130.2 24.7 %all-to-all-start.1 = ((f32[32,1,16]{2,1,0:T(1,128)}), f32[32,1,16]{2,1,0:T(1,128)S(1)}, u32[]{:S(2)}, u32[]{:S(2)}) async-start(f32[32,1,16]{2,1,0:T(1,128)} %bitcast.1), calls=%async_computation.1 | async-start | bytes 32768 | tf_op jit(solution)/shard_map/all_to_all | solution.py:15
  155.0 16.0 %all-to-all-start.2 = ((f32[32,128,16]{1,2,0:T(8,128)}), f32[32,128,16]{1,2,0:T(8,128)S(1)}, u32[]{:S(2)}, u32[]{:S(2)}) async-start(f32[32,128,16]{1,2,0:T(8,128)} %bitcast.3), calls=%async_computation.2 | async-start | bytes 524288 | tf_op jit(solution)/shard_map/all_to_all | solution.py:15
  171.8 13.5 %all-to-all-start.3 = ((f32[32,128,16]{1,2,0:T(8,128)}), f32[32,128,16]{1,2,0:T(8,128)S(1)}, u32[]{:S(2)}, u32[]{:S(2)}) async-start(f32[32,128,16]{1,2,0:T(8,128)} %broadcast_in_dim.5), calls=%async_computation.3 | async-start | bytes 524288 | tf_op jit(solution)/shard_map/all_to_all | solution.py:21
Sparse Core Ops, SparseCore 0:
  9.0 113.5 all-gather.2
  124.3 115.0 all-gather.4
where the time goes:
time: 262 us; the launch traced here: 261 us
  waiting for transfers between devices  157 us (60%)
  matrix products  47.1 us (18%)
  starting transfers between devices  30 us (11%)
  between operations  14.8 us (6%)
  other arithmetic  9.76 us (4%)
    all_gather x1, waiting for transfers between devices, on_device(): gathered = lax.all_gather(particles, 'dom', axis=0, tiled=True)  102 us
    all_gather x1, waiting for transfers between devices, on_device(): lax.all_gather(scores, 'dom', axis=0, tiled=True)  39.6 us
    dot_general x1, matrix products, on_device(): lax.dot_general(particles, gathered, (((1,), (1,)), ((), ())), precision=...  17.7 us
    all_to_all x2, starting transfers between devices, from_everyone(): lax.all_to_all(jnp.broadcast_to(array[None], (devices, *array.shape)), ax...  15.2 us
    dot_general x1, matrix products, on_device(): jnp.dot(kernel, lax.all_gather(scores, 'dom', axis=0, tiled=True), precis...  15 us
    all_to_all x2, starting transfers between devices, sum_at_owner(): lax.all_to_all(blocks, axis, split_axis=0, concat_axis=0, tiled=True)  14.8 us
    dot_general x1, matrix products, on_device(): jnp.dot(kernel, gathered, precision=precise, preferred_element_type=jnp.f...  14.4 us
    all_to_all x2, waiting for transfers between devices, sum_at_owner(): lax.all_to_all(blocks, axis, split_axis=0, concat_axis=0, tiled=True)  7.48 us
  transfers between devices with their start and end apart: 6, of which 4 were waited for; matrix products, arithmetic and copies ran while one was open for 17% of the time, Pallas kernels for 0%

commit v1 on v0

--- a/solution.py
+++ b/solution.py
@@ -59,7 +59,9 @@
     kernel = gathered_copies(kernel_share, "dim", 1)
     attract = jnp.dot(
         kernel,
-        lax.all_gather(scores, "dom", axis=0, tiled=True),
+        jnp.concatenate(
+            lax.all_to_all(jnp.stack([scores] * lax.axis_size("dom")), "dom", 0, 0), axis=0
+        ),
         precision=precise,
         preferred_element_type=jnp.float32,
     )

time: 262 us -> 408 us (1.56)
  waiting for transfers between devices: 157 us -> 279 us
  blocking collectives: 0 us -> 11.7 us
  local copies, waits for them, and re-layouts: 2.04 us -> 11.2 us
  starting transfers between devices: 30 us -> 34.6 us
    all_to_all x0 -> x1, waiting for transfers between devices: none -> 168 us  [on_device(): lax.all_to_all(jnp.stack([scores] * lax.axis_size('dom')), 'dom', 0, 0)]
    all_gather x1 -> x0, waiting for transfers between devices: 39.6 us -> none  [on_device(): lax.all_gather(scores, 'dom', axis=0, tiled=True)]
    all_to_all x0 -> x1, blocking collectives: none -> 11.7 us  [from_everyone(): lax.all_to_all(jnp.broadcast_to(array[None], (devices, *array.shape)), ax...]
    all_to_all x0 -> x1, starting transfers between devices: none -> 10.2 us  [on_device(): lax.all_to_all(jnp.stack([scores] * lax.axis_size('dom')), 'dom', 0, 0)]
    another operation x0 -> x1, local copies, waits for them, and re-layouts: none -> 9.91 us  [on_device(): jnp.stack([scores] * lax.axis_size('dom'))]
    all_to_all x2 -> x1, waiting for transfers between devices: 7.32 us -> 0.01 us  [from_everyone(): lax.all_to_all(jnp.broadcast_to(array[None], (devices, *array.shape)), ax...]
    all_to_all x2 -> x1, starting transfers between devices: 15.2 us -> 9.71 us  [from_everyone(): lax.all_to_all(jnp.broadcast_to(array[None], (devices, *array.shape)), ax...]
  transfers between devices with their start and end apart: 6 -> 5, of which waited for: 4 -> 3; matrix products, arithmetic and copies ran while one was open for 17% -> 10% of each run, Pallas kernels for 0% -> 0%
where the time goes in v1:
time: 408 us
  waiting for transfers between devices  279 us (68%)
  matrix products  46.3 us (11%)
  starting transfers between devices  34.6 us (8%)
  between operations  14.8 us (4%)
  blocking collectives  11.7 us (3%)
  local copies, waits for them, and re-layouts  11.2 us (3%)
  other arithmetic  9.76 us (2%)
    all_to_all x1, waiting for transfers between devices, on_device(): lax.all_to_all(jnp.stack([scores] * lax.axis_size('dom')), 'dom', 0, 0)  168 us
    all_gather x1, waiting for transfers between devices, on_device(): gathered = lax.all_gather(particles, 'dom', axis=0, tiled=True)  102 us
    dot_general x1, matrix products, on_device(): lax.dot_general(particles, gathered, (((1,), (1,)), ((), ())), precision=...  16.9 us
    dot_general x1, matrix products, on_device(): jnp.dot(kernel, jnp.concatenate(lax.all_to_all(jnp.stack([scores] * lax.a...  15 us
    all_to_all x2, starting transfers between devices, sum_at_owner(): lax.all_to_all(blocks, axis, split_axis=0, concat_axis=0, tiled=True)  14.7 us
    dot_general x1, matrix products, on_device(): jnp.dot(kernel, gathered, precision=precise, preferred_element_type=jnp.f...  14.4 us
    all_to_all x1, blocking collectives, from_everyone(): lax.all_to_all(jnp.broadcast_to(array[None], (devices, *array.shape)), ax...  11.7 us
    all_to_all x1, starting transfers between devices, on_device(): lax.all_to_all(jnp.stack([scores] * lax.axis_size('dom')), 'dom', 0, 0)  10.2 us
  transfers between devices with their start and end apart: 5, of which 3 were waited for; matrix products, arithmetic and copies ran while one was open for 10% of the time, Pallas kernels for 0%

profile of v1, /device:TPU:1, one launch (start us, length us, event | category | flops | bytes accessed | tf_op | source)
XLA Modules:
  0.0 407.5 jit_solution(8494197300338567674)
XLA Ops:
  6.5 0.0 all-gather.2.cloned.1.call-start
  6.5 0.7 all-gather.2.cloned.1.call-update
  7.3 2.5 multiply_reduce_fusion.1
  9.8 0.6 broadcast_in_dim.4
  10.4 9.7 %all-to-all-start = ((f32[32,1,128]{2,1,0:T(1,128)}), f32[32,1,128]{2,1,0:T(1,128)S(1)}, u32[]{:S(2)}, u32[]{:S(2)}) async-start(f32[32,1,128]{2,1,0:T(1,128)} %broadcast_in_dim.4), calls=%async_computation | async-start | bytes 32768 | tf_op jit(solution)/shard_map/all_to_all | solution.py:21
  20.1 102.4 %all-gather.2.cloned.1.call-done = f32[512,8192]{1,0:T(8,128)} async-done(((f32[128,8192]{1,0:T(8,128)}), f32[512,8192]{1,0:T(8,128)}) %all-gather.2.cloned.1.call-update) | async-done | bytes 16777232 | tf_op jit(solution)/shard_map/all_gather | solution.py:45
  122.6 7.0 %multiply_reduce_fusion = f32[512]{0:T(512)S(1)} fusion(f32[512,8192]{1,0:T(8,128)} %all-gather.2.cloned.1.call-done), kind=kLoop, calls=%fused_computation | loop fusion | flops 8388096 | bytes 16779264 | tf_op jit(solution)/shard_map/reduce_sum | solution.py:53
  129.6 0.7 all_to_all.20
  130.2 0.0 all-to-all-done
  130.2 7.0 %all-to-all-start.1 = ((f32[32,1,16]{2,1,0:T(1,128)}), f32[32,1,16]{2,1,0:T(1,128)S(1)}, u32[]{:S(2)}, u32[]{:S(2)}) async-start(f32[32,1,16]{2,1,0:T(1,128)} %bitcast.1), calls=%async_computation.1 | async-start | bytes 32768 | tf_op jit(solution)/shard_map/all_to_all | solution.py:15
  137.2 16.9 %fusion.3 = f32[128,512]{0,1:T(8,128)} fusion(f32[128,8192]{1,0:T(8,128)} %param.4, f32[512,8192]{1,0:T(8,128)} %all-gather.2.cloned.1.call-done), kind=kOutput, calls=%fused_computation.8 | convolution fusion | flops 6442450944 | bytes 21233664 | tf_op jit(solution)/shard_map/dot_general | solution.py:46
  154.2 0.0 all-to-all-done.1
  154.2 7.7 %all-to-all-start.2 = ((f32[32,128,16]{1,2,0:T(8,128)}), f32[32,128,16]{1,2,0:T(8,128)S(1)}, u32[]{:S(2)}, u32[]{:S(2)}) async-start(f32[32,128,16]{1,2,0:T(8,128)} %bitcast.3), calls=%async_computation.2 | async-start | bytes 524288 | tf_op jit(solution)/shard_map/all_to_all | solution.py:15
  162.6 0.1 reduce_sum.57
  162.6 7.5 %all-to-all-done.2 = f32[32,128,16]{1,2,0:T(8,128)S(1)} async-done(((f32[32,128,16]{1,2,0:T(8,128)}), f32[32,128,16]{1,2,0:T(8,128)S(1)}, u32[]{:S(2)}, u32[]{:S(2)}) %all-to-all-start.2) | async-done | bytes 262176 | tf_op jit(solution)/shard_map/all_to_all | solution.py:15
  170.1 0.1 divide_exponential_fusion
  170.2 11.7 %all_to_all.30 = f32[32,128,16]{1,2,0:T(8,128)S(1)} all-to-all(f32[32,128,16]{1,2,0:T(8,128)S(1)} %broadcast_in_dim.5), channel_id=1, replica_groups=mesh['dom'=4,'dim'=32] {'dim'}, dimensions={0} | all-to-all | bytes 524288 | tf_op jit(solution)/shard_map/all_to_all | solution.py:21
  181.9 9.9 %stack.2 = f32[4,128,8192]{2,1,0:T(8,128)} broadcast(f32[128,8192]{1,0:T(8,128)} %param.5), dimensions={1,2} | broadcast | bytes 20971520 | tf_op jit(solution)/shard_map/stack | solution.py:63
  191.9 10.2 %all-to-all-start.4 = ((f32[4,128,8192]{2,1,0:T(8,128)}), f32[4,128,8192]{2,1,0:T(8,128)}, u32[]{:S(2)}, u32[]{:S(2)}) async-start(f32[4,128,8192]{2,1,0:T(8,128)} %stack.2), calls=%async_computation.4 | async-start | bytes 33554432 | tf_op jit(solution)/shard_map/all_to_all | solution.py:63
  202.8 0.1 reduce_sum.59
  202.8 14.4 %fusion = f32[128,8192]{1,0:T(8,128)} fusion(f32[128,512]{0,1:T(8,128)S(1)} %bitcast.15, f32[512,8192]{1,0:T(8,128)} %all-gather.2.cloned.1.call-done, f32[128,8192]{1,0:T(8,128)} %param.4, f32[128]{0:T(128)S(1)} %reduce_sum.59, f32[]{:T(128)S(6)} %div.17), kind=kOutput, calls=%fused_computation.2 | convolution fusion | flops 6445596672 | bytes 25428484 | tf_op jit(solution)/shard_map/dot_general | solution.py:68
  217.2 168.4 %all-to-all-done.4 = f32[4,128,8192]{2,1,0:T(8,128)} async-done(((f32[4,128,8192]{2,1,0:T(8,128)}), f32[4,128,8192]{2,1,0:T(8,128)}, u32[]{:S(2)}, u32[]{:S(2)}) %all-to-all-start.4) | async-done | bytes 16777248 | tf_op jit(solution)/shard_map/all_to_all | solution.py:63
  385.7 15.0 %fusion.2 = f32[128,8192]{1,0:T(8,128)} fusion(f32[128,8192]{1,0:T(8,128)} %param.4, f32[128,8192]{1,0:T(8,128)} %fusion, f32[128,512]{0,1:T(8,128)S(1)} %bitcast.16, f32[512,8192]{1,0:T(8,128)} %bitcast.6, f32[]{:T(128)S(6)} %mul.46), kind=kOutput, calls=%fused_computation.5 | convolution fusion | flops 6445596672 | bytes 29622276 | tf_op jit(solution)/shard_map/dot_general | solution.py:60
  (3 shorter events, 0.1 us)
Async XLA Ops:
  6.5 116.1 %all-gather.2.cloned.1.call-start = ((), (), s32[]{:S(2)}) async-start(), calls=%async_computation.5 | async-start | bytes 20971520 | tf_op jit(solution)/shard_map/all_gather | solution.py:45
  10.4 119.8 %all-to-all-start = ((f32[32,1,128]{2,1,0:T(1,128)}), f32[32,1,128]{2,1,0:T(1,128)S(1)}, u32[]{:S(2)}, u32[]{:S(2)}) async-start(f32[32,1,128]{2,1,0:T(1,128)} %broadcast_in_dim.4), calls=%async_computation | async-start | bytes 32768 | tf_op jit(solution)/shard_map/all_to_all | solution.py:21
  130.2 23.9 %all-to-all-start.1 = ((f32[32,1,16]{2,1,0:T(1,128)}), f32[32,1,16]{2,1,0:T(1,128)S(1)}, u32[]{:S(2)}, u32[]{:S(2)}) async-start(f32[32,1,16]{2,1,0:T(1,128)} %bitcast.1), calls=%async_computation.1 | async-start | bytes 32768 | tf_op jit(solution)/shard_map/all_to_all | solution.py:15
  154.2 15.9 %all-to-all-start.2 = ((f32[32,128,16]{1,2,0:T(8,128)}), f32[32,128,16]{1,2,0:T(8,128)S(1)}, u32[]{:S(2)}, u32[]{:S(2)}) async-start(f32[32,128,16]{1,2,0:T(8,128)} %bitcast.3), calls=%async_computation.2 | async-start | bytes 524288 | tf_op jit(solution)/shard_map/all_to_all | solution.py:15
  191.9 193.8 %all-to-all-start.4 = ((f32[4,128,8192]{2,1,0:T(8,128)}), f32[4,128,8192]{2,1,0:T(8,128)}, u32[]{:S(2)}, u32[]{:S(2)}) async-start(f32[4,128,8192]{2,1,0:T(8,128)} %stack.2), calls=%async_computation.4 | async-start | bytes 33554432 | tf_op jit(solution)/shard_map/all_to_all | solution.py:63
Sparse Core Ops, SparseCore 0:
  9.0 113.5 all-gather.1
